TPU v7x, 32 devices: a whole 2x2x4 slice. The times are simulated.
32 devices in a mesh: groups: 2 (over x), seq: 16 (over z, y, core).
Axes of the slice: x: 2, y: 2, z: 4, core: 2. Of those that a mesh axis runs over, the one named last changes fastest.
Arguments:
- queries: bfloat16 [1024, 2048], P(('groups', 'seq')), parts along dimension 0, may hold values from -132 to 132
- fresh_keys: bfloat16 [1024, 2048], P(('groups', 'seq')), parts along dimension 0, may hold values from -6 to 6
- fresh_values: bfloat16 [1024, 2048], P(('groups', 'seq')), parts along dimension 0, may hold values from -48 to 48
- stale_keys: bfloat16 [1024, 2048], P(('groups', 'seq')), parts along dimension 0, may hold values from -6 to 6
- stale_values: bfloat16 [1024, 2048], P(('groups', 'seq')), parts along dimension 0, may hold values from -48 to 48
- patch_sizes: int32 [8], P('groups'), parts along dimension 0, may hold values from 1 to 256, 512 in all
Outputs:
- attended: bfloat16 [1024, 2048], P(('groups', 'seq')), parts along dimension 0
There are 2 independent parts, one for each index of `groups`. A program takes and returns all parts, laid end to end along the dimension named above; each array names one. Nothing has to cross between parts.
Inputs may be any that keep to these rules, and one draw needn't show every extreme that they name: `patch_sizes`: the patch lengths sum to 512.
All inputs are finite; a program needn't handle non-finite values.
Results may differ from a plain program's by a relative error of at most 0.006.
Values may be sent and summed in bfloat16 or wider, within the bound.
A program may use at most 64 MiB of HBM per device.

v0:
```python
import functools

import jax
import jax.numpy as jnp
from jax import lax
from jax.experimental import pallas as pl
from jax.experimental.pallas import tpu as pltpu
from jax.sharding import PartitionSpec as P

H = 16
MESH = pl.DeviceIdType.MESH


def each(count, body):
    if count <= 32:
        for k in range(1, count):
            body(k)
    else:
        lax.fori_loop(1, count, lambda k, c: (body(k), c)[1], 0)


def flipped(me, k, count):
    if count & (count - 1):
        return lax.rem(me + k, count)
    peer, bit = 0, 1
    while bit < count:
        peer = peer + bit * lax.rem(me // bit + k // bit, 2)
        bit *= 2
    return peer


def kernel(
    n, fk_ref, sk_ref, fv_ref, sv_ref, q_ref, sizes_ref, out_ref,
    stage, got_q, got_kv, att,
    load_sem, own_sem, send_sem, recv_sem, back_send, back_recv,
):
    rows, columns = q_ref.shape
    hd = columns // H
    me = lax.axis_index("seq")
    head = lax.rem(me, H)
    base = me - head
    keys = n * rows
    queries = H * rows

    loads = []
    for i, ref in enumerate((fk_ref, sk_ref, fv_ref, sv_ref, q_ref)):
        c = pltpu.make_async_copy(ref, stage.at[i], load_sem.at[i])
        c.start()
        loads.append(c)

    barrier = pltpu.get_barrier_semaphore()
    each(n, lambda k: pl.semaphore_signal(
        barrier, inc=1, device_id={"seq": flipped(me, k, n)}, device_id_type=MESH))
    pl.semaphore_wait(barrier, n - 1)

    def cols(h):
        return pl.ds(pl.multiple_of(h * hd, hd), hd)

    def at(p):
        return pl.ds(pl.multiple_of(p * rows, rows), rows)

    def views(phase, peer_head, source):
        if phase == 0:
            return stage.at[0:4, :, cols(peer_head)], got_kv.at[:, at(source), :]
        return stage.at[4, :, cols(peer_head)], got_q.at[at(lax.rem(source, H)), :]

    def remote(phase, peer, source, slot):
        src, dst = views(phase, lax.rem(peer, H), source)
        return pltpu.make_async_remote_copy(
            src_ref=src, dst_ref=dst,
            send_sem=send_sem.at[phase, slot], recv_sem=recv_sem.at[phase, slot],
            device_id={"seq": peer}, device_id_type=MESH)

    def own(phase):
        src, dst = views(phase, head, me)
        return pltpu.make_async_copy(src, dst, own_sem.at[phase])

    loads[4].wait()
    each(H, lambda k: remote(1, base + flipped(head, k, H), me, k).start())
    own(1).start()
    for i in range(4):
        loads[i].wait()
    each(n, lambda k: remote(0, flipped(me, k, n), me, k).start())
    own(0).start()

    ends, total = [], 0
    for p in range(sizes_ref.shape[0] - 1):
        total = total + sizes_ref[p]
        ends.append(total)

    block = 4 * rows
    scale = hd ** (-0.5)
    contract = (((1,), (1,)), ((), ()))

    def attend(b):
        at_b = pl.ds(pl.multiple_of(b * block, block), block)
        token = base * rows + b * block + lax.broadcasted_iota(jnp.int32, (block, 1), 0)
        limit = jnp.full((block, 1), keys, jnp.int32)
        for e in reversed(ends):
            limit = jnp.where(token < e, e, limit)
        fresh = lax.broadcasted_iota(jnp.int32, (block, keys), 1) < limit
        qb = got_q[at_b, :]
        sf = lax.dot_general(qb, got_kv[0], contract, preferred_element_type=jnp.float32)
        ss = lax.dot_general(qb, got_kv[1], contract, preferred_element_type=jnp.float32)
        s = jnp.where(fresh, sf, ss)
        w = jnp.exp((s - jnp.max(s, axis=1, keepdims=True)) * scale)
        den = jnp.sum(w, axis=1, keepdims=True)
        zero = jnp.zeros_like(w)
        wf = jnp.where(fresh, w, zero).astype(jnp.bfloat16)
        ws = jnp.where(fresh, zero, w).astype(jnp.bfloat16)
        num = jnp.dot(wf, got_kv[2], preferred_element_type=jnp.float32)
        num = num + jnp.dot(ws, got_kv[3], preferred_element_type=jnp.float32)
        att[at_b, :] = (num / den).astype(jnp.bfloat16)

    def back(slot):
        j = flipped(head, slot, H)
        return pltpu.make_async_remote_copy(
            src_ref=att.at[at(j), :], dst_ref=out_ref.at[:, cols(head)],
            send_sem=back_send.at[slot], recv_sem=back_recv.at[slot],
            device_id={"seq": base + j}, device_id_type=MESH)

    back_own = pltpu.make_async_copy(att.at[at(head), :], out_ref.at[:, cols(head)], own_sem.at[2])

    each(n, lambda k: remote(0, me, me, k).wait_recv())
    own(0).wait()
    for k in (2, 3, 1, 0):
        for slot in range(4 * k, 4 * k + 4):
            if slot:
                remote(1, me, me, slot).wait_recv()
            else:
                own(1).wait()
        attend(flipped(head // 4, k, H // 4))
        for slot in range(4 * k, 4 * k + 4):
            if slot:
                back(slot).start()
            else:
                back_own.start()

    each(n, lambda k: remote(0, me, me, k).wait_send())
    each(H, lambda k: remote(1, me, me, k).wait_send())
    for slot in range(1, H):
        back(slot).wait()
    back_own.wait()


def shards(queries, fresh_keys, fresh_values, stale_keys, stale_values, patch_sizes):
    rows, columns = queries.shape
    n = lax.axis_size("seq")
    hd = columns // H
    keys, count = n * rows, H * rows
    dma = pltpu.SemaphoreType.DMA
    any_spec = pl.BlockSpec(memory_space=pl.ANY)
    return pl.pallas_call(
        functools.partial(kernel, n),
        out_shape=pltpu.VMEM((rows, columns), queries.dtype),
        in_specs=[any_spec] * 5 + [pl.BlockSpec(memory_space=pltpu.SMEM)],
        out_specs=pl.BlockSpec(memory_space=pltpu.VMEM),
        scratch_shapes=[
            pltpu.VMEM((5, rows, columns), queries.dtype),
            pltpu.VMEM((count, hd), queries.dtype),
            pltpu.VMEM((4, keys, hd), queries.dtype),
            pltpu.VMEM((count, hd), queries.dtype),
            dma((5,)), dma((3,)), dma((2, n)), dma((2, n)), dma((H,)), dma((H,)),
        ],
        compiler_params=pltpu.CompilerParams(collective_id=0, has_side_effects=True),
    )(fresh_keys, stale_keys, fresh_values, stale_values, queries, patch_sizes)


def solution(mesh):
    spec = P(("groups", "seq"), None)
    return jax.shard_map(
        shards, mesh=mesh, in_specs=(spec,) * 5 + (P("groups"),), out_specs=spec, check_vma=False)
```

profile of v0, /device:TPU:0, one launch (start us, length us, event | category | flops | bytes accessed | tf_op | source)
XLA Modules:
  0.0 29.1 jit_solution(5799988589896840714)
XLA Ops:
  0.0 28.4 %shard_map.64 = bf16[32,2048]{1,0:T(8,128)(2,1)S(1)} custom-call(bf16[32,2048]{1,0:T(8,128)(2,1)} %fk_ref.1, bf16[32,2048]{1,0:T(8,128)(2,1)} %sk_ref.1, bf16[32,2048]{1,0:T(8,128)(2,1)} %fv_ref.1, bf16[32,2048]{1,0:T(8,128)(2,1)} %sv_ref.1, bf16[32,2048]{1,0:T(8,128)(2,1)} %q_ref.1, s32[4]{0:T(128)} %sizes_ref.1), custom_call_target="tpu_custom_call" | custom-call | tf_op jit(solution)/shard_map/pallas_call | solution.py:153
  28.4 0.7 %copy.8 = bf16[32,2048]{1,0:T(8,128)(2,1)} copy(bf16[32,2048]{1,0:T(8,128)(2,1)S(1)} %shard_map.64) | data formatting | bytes 262144
where the time goes:
time: 29.2 us; the launch traced here: 29.1 us
  Pallas kernels  28.4 us (97%)
  local copies, waits for them, and re-layouts  0.66 us (2%)
    pallas_call x1, Pallas kernels, shards(): pl.pallas_call(functools.partial(kernel, n), out_shape=pltpu.VMEM((rows,...  28.4 us
    unnamed x1, local copies, waits for them, and re-layouts  0.66 us

commit v1 on v0

--- a/solution.py
+++ b/solution.py
@@ -29,7 +29,7 @@
     return peer
 
 
-def kernel(
+def spread_kernel(
     n, fk_ref, sk_ref, fv_ref, sv_ref, q_ref, sizes_ref, out_ref,
     stage, got_q, got_kv, att,
     load_sem, own_sem, send_sem, recv_sem, back_send, back_recv,
@@ -143,7 +143,7 @@
     back_own.wait()
 
 
-def shards(queries, fresh_keys, fresh_values, stale_keys, stale_values, patch_sizes):
+def spread_shards(queries, fresh_keys, fresh_values, stale_keys, stale_values, patch_sizes):
     rows, columns = queries.shape
     n = lax.axis_size("seq")
     hd = columns // H
@@ -151,7 +151,7 @@
     dma = pltpu.SemaphoreType.DMA
     any_spec = pl.BlockSpec(memory_space=pl.ANY)
     return pl.pallas_call(
-        functools.partial(kernel, n),
+        functools.partial(spread_kernel, n),
         out_shape=pltpu.VMEM((rows, columns), queries.dtype),
         in_specs=[any_spec] * 5 + [pl.BlockSpec(memory_space=pltpu.SMEM)],
         out_specs=pl.BlockSpec(memory_space=pltpu.VMEM),
@@ -166,7 +166,184 @@
     )(fresh_keys, stale_keys, fresh_values, stale_values, queries, patch_sizes)
 
 
+def wave(i):
+    return i // 4 + lax.rem(i // 2, 2)
+
+
+def kernel(
+    n, fk_ref, sk_ref, fv_ref, sv_ref, q_ref, sizes_hbm, out_ref,
+    stage, got_q, got_kv, att, sizes_ref,
+    load_sem, own_sem, send_sem, recv_sem, back_send, back_recv, ready,
+):
+    rows, columns = q_ref.shape
+    hd = columns // H
+    me = lax.axis_index("seq")
+    keys = n * rows
+
+    loads = []
+    for i, ref in enumerate((fk_ref, sk_ref, fv_ref, sv_ref, q_ref)):
+        c = pltpu.make_async_copy(ref, stage.at[i], load_sem.at[i])
+        c.start()
+        loads.append(c)
+    load_sizes = pltpu.make_async_copy(sizes_hbm, sizes_ref, load_sem.at[5])
+    load_sizes.start()
+
+    def signal(sem, peer):
+        pl.semaphore_signal(sem, inc=1, device_id={"seq": peer}, device_id_type=MESH)
+
+    def others(body, far=False):
+        for d in (range(n - 1, 0, -1) if far else range(1, n)):
+            for peer, there in ((me + d, me + d < n), (me - d, me >= d)):
+                body(jnp.where(there, peer, me), there)
+
+    mine = wave(me)
+    barrier = pltpu.get_barrier_semaphore()
+
+    def greet(peer, there):
+        pl.when(there & (wave(peer) >= mine))(lambda: signal(barrier, peer))
+
+    others(greet)
+    pl.semaphore_wait(barrier, jnp.minimum(4 * mine + 2, n) - 1)
+
+    def answer(peer, there):
+        pl.when(there & (wave(peer) < mine))(lambda: signal(ready.at[me], peer))
+
+    others(answer)
+
+    def cols(h):
+        return pl.ds(pl.multiple_of(h * hd, hd), hd)
+
+    def at(p):
+        return pl.ds(pl.multiple_of(p * rows, rows), rows)
+
+    def views(phase, peer, source):
+        if phase == 0:
+            return stage.at[0:4, :, cols(peer)], got_kv.at[:, at(source), :]
+        return stage.at[4, :, cols(peer)], got_q.at[at(source), :]
+
+    def remote(phase, peer, source, slot):
+        src, dst = views(phase, peer, source)
+        return pltpu.make_async_remote_copy(
+            src_ref=src, dst_ref=dst,
+            send_sem=send_sem.at[phase, peer], recv_sem=recv_sem.at[phase, slot],
+            device_id={"seq": peer}, device_id_type=MESH)
+
+    def own(phase):
+        src, dst = views(phase, me, me)
+        return pltpu.make_async_copy(src, dst, own_sem.at[phase])
+
+    for i in range(4):
+        loads[i].wait()
+
+    def send_met(peer, there):
+        pl.when(there & (wave(peer) <= mine))(lambda: remote(0, peer, me, me).start())
+
+    def send_later(peer, there):
+        def go():
+            pl.semaphore_wait(ready.at[peer], 1)
+            remote(0, peer, me, me).start()
+
+        pl.when(there & (wave(peer) > mine))(go)
+
+    def send_q(peer, there):
+        pl.when(there)(lambda: remote(1, peer, me, me).start())
+
+    others(send_met, far=True)
+    others(send_later)
+    loads[4].wait()
+    others(send_q)
+    own(0).start()
+    own(1).start()
+    load_sizes.wait()
+
+    ends, total = [], 0
+    for p in range(sizes_ref.shape[0] - 1):
+        total = total + sizes_ref[p]
+        ends.append(total)
+
+    block = 4 * rows
+    scale = hd ** (-0.5)
+    contract = (((1,), (1,)), ((), ()))
+
+    def attend(b):
+        at_b = pl.ds(b * block, block)
+        token = b * block + lax.broadcasted_iota(jnp.int32, (block, 1), 0)
+        limit = jnp.full((block, 1), keys, jnp.int32)
+        for e in reversed(ends):
+            limit = jnp.where(token < e, e, limit)
+        fresh = lax.broadcasted_iota(jnp.int32, (block, keys), 1) < limit
+        qb = got_q[at_b, :]
+        sf = lax.dot_general(qb, got_kv[0], contract, preferred_element_type=jnp.float32)
+        ss = lax.dot_general(qb, got_kv[1], contract, preferred_element_type=jnp.float32)
+        s = jnp.where(fresh, sf, ss)
+        w = jnp.exp((s - jnp.max(s, axis=1, keepdims=True)) * scale)
+        den = jnp.sum(w, axis=1, keepdims=True)
+        zero = jnp.zeros_like(w)
+        wf = jnp.where(fresh, w, zero).astype(jnp.bfloat16)
+        ws = jnp.where(fresh, zero, w).astype(jnp.bfloat16)
+        num = jnp.dot(wf, got_kv[2], preferred_element_type=jnp.float32)
+        num = num + jnp.dot(ws, got_kv[3], preferred_element_type=jnp.float32)
+        att[at_b, :] = (num / den).astype(jnp.bfloat16)
+
+    def back(peer, source):
+        return pltpu.make_async_remote_copy(
+            src_ref=att.at[at(peer), :], dst_ref=out_ref.at[:, cols(source)],
+            send_sem=back_send.at[peer], recv_sem=back_recv.at[source],
+            device_id={"seq": peer}, device_id_type=MESH)
+
+    back_own = pltpu.make_async_copy(att.at[at(me), :], out_ref.at[:, cols(me)], own_sem.at[2])
+
+    def by_peer(sources, body, mine):
+        for j in sources:
+            pl.when(me != j)(functools.partial(body, j))
+            pl.when(me == j)(mine)
+
+    by_peer(range(n), lambda j: remote(0, me, j, j).wait_recv(), own(0).wait)
+    for b in range(n // 4):
+        group = range(4 * b, 4 * b + 4)
+        by_peer(group, lambda j: remote(1, me, j, j).wait_recv(), own(1).wait)
+        attend(b)
+        by_peer(group, lambda j: back(j, me).start(), back_own.start)
+
+    def drain(peer, there):
+        def go():
+            remote(0, peer, me, me).wait_send()
+            remote(1, peer, me, me).wait_send()
+            back(peer, me).wait_send()
+            back(me, peer).wait_recv()
+
+        pl.when(there)(go)
+
+    others(drain)
+    back_own.wait()
+
+
+def shards(queries, fresh_keys, fresh_values, stale_keys, stale_values, patch_sizes):
+    rows, columns = queries.shape
+    n = lax.axis_size("seq")
+    hd = columns // H
+    keys = n * rows
+    dma = pltpu.SemaphoreType.DMA
+    return pl.pallas_call(
+        functools.partial(kernel, n),
+        out_shape=pltpu.VMEM((rows, columns), queries.dtype),
+        in_specs=[pl.BlockSpec(memory_space=pl.ANY)] * 6,
+        out_specs=pl.BlockSpec(memory_space=pltpu.VMEM),
+        scratch_shapes=[
+            pltpu.VMEM((5, rows, columns), queries.dtype),
+            pltpu.VMEM((keys, hd), queries.dtype),
+            pltpu.VMEM((4, keys, hd), queries.dtype),
+            pltpu.VMEM((keys, hd), queries.dtype),
+            pltpu.SMEM(patch_sizes.shape, patch_sizes.dtype),
+            dma((6,)), dma((3,)), dma((2, n)), dma((2, n)), dma((n,)), dma((n,)),
+            pltpu.SemaphoreType.REGULAR((n,)),
+        ],
+        compiler_params=pltpu.CompilerParams(collective_id=0, has_side_effects=True),
+    )(fresh_keys, stale_keys, fresh_values, stale_values, queries, patch_sizes)
+
+
 def solution(mesh):
     spec = P(("groups", "seq"), None)
+    body = shards if mesh.shape["seq"] == H else spread_shards
     return jax.shard_map(
-        shards, mesh=mesh, in_specs=(spec,) * 5 + (P("groups"),), out_specs=spec, check_vma=False)
+        body, mesh=mesh, in_specs=(spec,) * 5 + (P("groups"),), out_specs=spec, check_vma=False)

time: 29.2 us -> 26.9 us (0.921)
  Pallas kernels: 28.4 us -> 26.1 us
    pallas_call x1, Pallas kernels: 28.4 us -> 26.1 us  [shards(): pl.pallas_call(functools.partial(kernel, n), out_shape=pltpu.VMEM((rows,...]
where the time goes in v1:
time: 26.9 us; the launch traced here: 26.8 us
  Pallas kernels  26.1 us (97%)
  local copies, waits for them, and re-layouts  0.66 us (2%)
    pallas_call x1, Pallas kernels, shards(): pl.pallas_call(functools.partial(kernel, n), out_shape=pltpu.VMEM((rows,...  26.1 us
    unnamed x1, local copies, waits for them, and re-layouts  0.66 us

profile of v1, /device:TPU:0, one launch (start us, length us, event | category | flops | bytes accessed | tf_op | source)
XLA Modules:
  0.0 26.8 jit_solution(17506908197172851278)
XLA Ops:
  0.0 26.1 %shard_map.64 = bf16[32,2048]{1,0:T(8,128)(2,1)S(1)} custom-call(bf16[32,2048]{1,0:T(8,128)(2,1)} %fk_ref.1, bf16[32,2048]{1,0:T(8,128)(2,1)} %sk_ref.1, bf16[32,2048]{1,0:T(8,128)(2,1)} %fv_ref.1, bf16[32,2048]{1,0:T(8,128)(2,1)} %sv_ref.1, bf16[32,2048]{1,0:T(8,128)(2,1)} %q_ref.1, s32[4]{0:T(128)} %sizes_hbm.1), custom_call_target="tpu_custom_call" | custom-call | tf_op jit(solution)/shard_map/pallas_call | solution.py:327
  26.1 0.7 %copy.8 = bf16[32,2048]{1,0:T(8,128)(2,1)} copy(bf16[32,2048]{1,0:T(8,128)(2,1)S(1)} %shard_map.64) | data formatting | bytes 262144

commit v2 on v0

--- a/solution.py
+++ b/solution.py
@@ -29,7 +29,7 @@
     return peer
 
 
-def kernel(
+def spread_kernel(
     n, fk_ref, sk_ref, fv_ref, sv_ref, q_ref, sizes_ref, out_ref,
     stage, got_q, got_kv, att,
     load_sem, own_sem, send_sem, recv_sem, back_send, back_recv,
@@ -143,7 +143,7 @@
     back_own.wait()
 
 
-def shards(queries, fresh_keys, fresh_values, stale_keys, stale_values, patch_sizes):
+def spread_shards(queries, fresh_keys, fresh_values, stale_keys, stale_values, patch_sizes):
     rows, columns = queries.shape
     n = lax.axis_size("seq")
     hd = columns // H
@@ -151,7 +151,7 @@
     dma = pltpu.SemaphoreType.DMA
     any_spec = pl.BlockSpec(memory_space=pl.ANY)
     return pl.pallas_call(
-        functools.partial(kernel, n),
+        functools.partial(spread_kernel, n),
         out_shape=pltpu.VMEM((rows, columns), queries.dtype),
         in_specs=[any_spec] * 5 + [pl.BlockSpec(memory_space=pltpu.SMEM)],
         out_specs=pl.BlockSpec(memory_space=pltpu.VMEM),
@@ -166,7 +166,283 @@
     )(fresh_keys, stale_keys, fresh_values, stale_values, queries, patch_sizes)
 
 
+def kernel(
+    n, fk_ref, sk_ref, fv_ref, sv_ref, q_ref, sizes_hbm, out_ref,
+    stage, got_q, got_kv, turned, att, lse_out, part, lse_in, mix, sizes_ref,
+    load_sem, kv_recv, q_recv, o_recv, l_recv, kv_send, q_send, o_send, l_send, ready,
+):
+    rows, columns = q_ref.shape
+    hd = columns // H
+    me = lax.axis_index("seq")
+    half = n // 2
+    held = H // half
+    keys = half * rows
+    lanes = lse_in.shape[2]
+    per = lanes // rows
+    chips = n // 2
+    side = me // half
+
+    for i, ref in enumerate((fk_ref, sk_ref, fv_ref, sv_ref, q_ref)):
+        pltpu.make_async_copy(ref, stage.at[i], load_sem.at[0]).start()
+    load_sizes = pltpu.make_async_copy(sizes_hbm, sizes_ref, load_sem.at[1])
+    load_sizes.start()
+
+    def wave(i):
+        return i // 4 + lax.rem(i // 2, 2)
+
+    def signal(sem, peer):
+        pl.semaphore_signal(sem, inc=1, device_id={"seq": peer}, device_id_type=MESH)
+
+    mine, chip = wave(me), me // 2
+    upper = lax.rem(chip, 2) == 1
+    buddy = 2 * chip + 1 - lax.rem(me, 2)
+    barrier = pltpu.get_barrier_semaphore()
+    signal(barrier, buddy)
+    for d in range(1, n):
+        peer = me + d
+        pl.when((peer < n) & (wave(peer) > mine))(functools.partial(signal, barrier, jnp.where(peer < n, peer, me)))
+    pl.semaphore_wait(barrier, jnp.maximum(4 * mine - 2, 0) + 1)
+    for d in range(1, n):
+        peer = me - d
+        pl.when((peer >= 0) & (wave(peer) < mine))(functools.partial(signal, ready.at[chip], jnp.maximum(peer, 0)))
+
+    def cols(h, count=1):
+        return pl.ds(pl.multiple_of(h * hd, hd), count * hd)
+
+    def at(p, count=1):
+        return pl.ds(pl.multiple_of(p * rows, rows), count * rows)
+
+    def to(peer, src, dst, send, recv):
+        return pltpu.make_async_remote_copy(
+            src_ref=src, dst_ref=dst, send_sem=send, recv_sem=recv,
+            device_id={"seq": peer}, device_id_type=MESH)
+
+    def kv_views(a, peer):
+        return (stage.at[0:4, :, cols(lax.rem(peer, half) * held + a)],
+                got_kv.at[a, :, at(lax.rem(me, half)), :])
+
+    def q_views(peer):
+        return stage.at[4, :, cols(lax.rem(peer, half) * held, held)], got_q.at[at(me), :]
+
+    def o_views(a, peer):
+        return (att.at[at(peer), a * hd:(a + 1) * hd],
+                part.at[side, :, cols(lax.rem(me, half) * held + a)])
+
+    def l_views(peer):
+        return lse_out.at[peer // per], lse_in.at[me]
+
+    def send_kv(a, peer):
+        to(peer, *kv_views(a, peer), kv_send.at[0], kv_recv.at[a]).start()
+
+    def send_q(peer):
+        to(peer, *q_views(peer), q_send.at[0], q_recv.at[side]).start()
+
+    def send_o(a, peer):
+        to(peer, *o_views(a, peer), o_send.at[0], o_recv.at[0]).start()
+
+    def send_l(peer):
+        to(peer, *l_views(peer), l_send.at[0], l_recv.at[0]).start()
+
+    def arrived(sem, ref):
+        to(me, ref, ref, sem, sem).wait_recv()
+
+    def left(sem, ref):
+        to(me, ref, ref, sem, sem).wait_send()
+
+    def keep(src, dst):
+        dst[...] = src[...]
+
+    def cores(target, cond, body):
+        @pl.when(cond)
+        def _():
+            for core in range(2):
+                body(2 * jnp.clip(target, 0, chips - 1) + core)
+
+    def near(target):
+        return target // (chips // 2) == side
+
+    def tied(target):
+        return (upper & (target == chip + 1)) | (jnp.logical_not(upper) & (target == chip - 1))
+
+    def met(body, same):
+        for e in range(1, chips):
+            t = chip - e
+            cores(t, (t >= 0) & jnp.logical_not(tied(t)) & (near(t) == same), body)
+
+    def heard(body):
+        for e in range(1, chips):
+            t = chip + e
+            cores(t, (t < chips) & jnp.logical_not(tied(t)) & near(t), body)
+        for t in (chip - 1, chip + 1):
+            cores(t, (t >= 0) & (t < chips) & tied(t) & near(t), body)
+
+    arrived(load_sem.at[0], stage)
+    def met_q():
+        send_q(buddy)
+        met(send_q, True)
+
+    for a in range(held):
+        send_kv(a, buddy)
+        met(functools.partial(send_kv, a), True)
+        if a == 0:
+            pl.when(side == 0)(met_q)
+    met(send_q, False)
+
+    def first(target, cond):
+        cores(target, cond & near(target), functools.partial(send_kv, 0))
+        cores(target, cond & ((side == 0) | jnp.logical_not(near(target))), send_q)
+
+    for e in range(1, chips):
+        t = chip + e
+        there = (t < chips) & jnp.logical_not(tied(t))
+
+        @pl.when(there)
+        def _():
+            pl.semaphore_wait(ready.at[t], 2)
+
+        first(t, there)
+        if e == 1:
+            t = chip - 1
+            first(t, (t >= 0) & tied(t))
+        if e == 2:
+            t = chip + 1
+            first(t, (t < chips) & tied(t))
+    for a in range(1, held):
+        heard(functools.partial(send_kv, a))
+
+    def late_q():
+        met_q()
+        heard(send_q)
+
+    pl.when(side == 1)(late_q)
+    for a in range(held):
+        keep(*kv_views(a, me))
+    keep(*q_views(me))
+    load_sizes.wait()
+
+    ends, total = [], 0
+    for p in range(sizes_ref.shape[0] - 1):
+        total = total + sizes_ref[p]
+        ends.append(total)
+
+    scale = hd ** (-0.5) * 1.4426950408889634
+    contract = (((1,), (1,)), ((), ()))
+
+    def turn(a):
+        turned[a, :, 0:keys] = got_kv[a, 2].T
+        turned[a, :, keys:2 * keys] = got_kv[a, 3].T
+
+    def attend(a, s):
+        token = s * keys + lax.broadcasted_iota(jnp.int32, (1, keys), 1)
+        limit = jnp.full((1, keys), 2 * keys, jnp.int32)
+        for e in reversed(ends):
+            limit = jnp.where(token < e, e, limit)
+        fresh = lax.broadcasted_iota(jnp.int32, (keys, keys), 0) < limit - side * keys
+        both = got_kv[a, 0:2].reshape(2 * keys, hd)
+        qb = got_q[s * keys:(s + 1) * keys, a * hd:(a + 1) * hd]
+        x = lax.dot_general(both, qb, contract, preferred_element_type=jnp.float32)
+        x = jnp.where(fresh, x[:keys], x[keys:])
+        top = jnp.max(x, axis=0, keepdims=True)
+        w = jnp.exp2((x - top) * scale)
+        den = jnp.sum(w, axis=0, keepdims=True)
+        zero = jnp.zeros_like(w)
+        wf = jnp.where(fresh, w, zero).astype(jnp.bfloat16)
+        ws = jnp.where(fresh, zero, w).astype(jnp.bfloat16)
+        num = jnp.dot(turned[a], jnp.concatenate([wf, ws], axis=0), preferred_element_type=jnp.float32)
+        att[s * keys:(s + 1) * keys, a * hd:(a + 1) * hd] = (num * (1.0 / den)).T.astype(jnp.bfloat16)
+        lse = top * scale + jnp.log2(den)
+        for b in range(keys // lanes):
+            lse_out[s * (keys // lanes) + b, a:a + 1, :] = lse[:, b * lanes:(b + 1) * lanes]
+
+    def give(s, body, own):
+        for j in range(s * half, (s + 1) * half):
+            pl.when(me != j)(functools.partial(body, j))
+        pl.when(side == s)(own)
+
+    def give_o(a, s):
+        give(s, functools.partial(send_o, a), lambda: keep(*o_views(a, me)))
+
+    def give_l(s):
+        give(s, send_l, lambda: keep(*l_views(me)))
+
+    def wait_q(s):
+        pl.when(side == s)(lambda: arrived(q_recv.at[s], got_q.at[0:(half - 1) * rows, :]))
+        pl.when(side != s)(lambda: arrived(q_recv.at[s], got_q.at[0:half * rows, :]))
+
+    for a in range(held):
+        arrived(kv_recv.at[a], got_kv.at[a, :, 0:(half - 1) * rows, :])
+        turn(a)
+        if a == 0:
+            wait_q(0)
+        attend(a, 0)
+        if a == held - 1:
+            give_l(0)
+        give_o(a, 0)
+    wait_q(1)
+    for a in range(held):
+        attend(a, 1)
+        if a == held - 1:
+            give_l(1)
+        give_o(a, 1)
+
+    most = (n - 1) * rows
+    arrived(o_recv.at[0], att.at[0:most, :])
+    arrived(l_recv.at[0], lse_in.at[0:n - 1])
+    low = lse_in[0:half].reshape(H, lanes)
+    high = lse_in[half:n].reshape(H, lanes)
+    top = jnp.maximum(low, high)
+    low, high = jnp.exp2(low - top), jnp.exp2(high - top)
+    total = low + high
+    fill = jnp.zeros((lanes - 2 * H, lanes), jnp.float32)
+    mix[...] = jnp.concatenate([low / total, high / total, fill], axis=0).T
+    share = mix[at(lax.rem(me, per)), :]
+    for h in range(H):
+        c = slice(h * hd, (h + 1) * hd)
+        out = share[:, h:h + 1] * part[0, :, c].astype(jnp.float32)
+        out = out + share[:, H + h:H + h + 1] * part[1, :, c].astype(jnp.float32)
+        out_ref[:, c] = out.astype(out_ref.dtype)
+
+    left(kv_send.at[0], got_kv.at[:, :, 0:(half - 1) * rows, :])
+    left(q_send.at[0], got_q.at[0:most, :])
+    left(o_send.at[0], att.at[0:most, :])
+    left(l_send.at[0], lse_in.at[0:n - 1])
+
+
+def shards(queries, fresh_keys, fresh_values, stale_keys, stale_values, patch_sizes):
+    rows, columns = queries.shape
+    n = lax.axis_size("seq")
+    hd = columns // H
+    half = n // 2
+    held = H // half
+    keys, lanes = half * rows, 128
+    dma = pltpu.SemaphoreType.DMA
+    kind = queries.dtype
+    return pl.pallas_call(
+        functools.partial(kernel, n),
+        out_shape=pltpu.VMEM((rows, columns), kind),
+        in_specs=[pl.BlockSpec(memory_space=pl.ANY)] * 6,
+        out_specs=pl.BlockSpec(memory_space=pltpu.VMEM),
+        scratch_shapes=[
+            pltpu.VMEM((5, rows, columns), kind),
+            pltpu.VMEM((n * rows, held * hd), kind),
+            pltpu.VMEM((held, 4, keys, hd), kind),
+            pltpu.VMEM((held, hd, 2 * keys), kind),
+            pltpu.VMEM((n * rows, held * hd), kind),
+            pltpu.VMEM((n * rows // lanes, held, lanes), jnp.float32),
+            pltpu.VMEM((2, rows, columns), kind),
+            pltpu.VMEM((n, held, lanes), jnp.float32),
+            pltpu.VMEM((lanes, lanes), jnp.float32),
+            pltpu.SMEM(patch_sizes.shape, patch_sizes.dtype),
+            dma((2,)), dma((held,)), dma((2,)), dma((1,)), dma((1,)),
+            dma((1,)), dma((1,)), dma((1,)), dma((1,)),
+            pltpu.SemaphoreType.REGULAR((n // 2,)),
+        ],
+        compiler_params=pltpu.CompilerParams(collective_id=0, has_side_effects=True),
+    )(fresh_keys, stale_keys, fresh_values, stale_values, queries, patch_sizes)
+
+
 def solution(mesh):
     spec = P(("groups", "seq"), None)
+    body = shards if mesh.shape["seq"] == H else spread_shards
     return jax.shard_map(
-        shards, mesh=mesh, in_specs=(spec,) * 5 + (P("groups"),), out_specs=spec, check_vma=False)
+        body, mesh=mesh, in_specs=(spec,) * 5 + (P("groups"),), out_specs=spec, check_vma=False)

time: 29.2 us -> 24.2 us (0.83)
  Pallas kernels: 28.4 us -> 23.3 us
    pallas_call x1, Pallas kernels: 28.4 us -> 23.3 us  [shards(): pl.pallas_call(functools.partial(kernel, n), out_shape=pltpu.VMEM((rows,...]
where the time goes in v2:
time: 24.2 us; the launch traced here: 24 us
  Pallas kernels  23.3 us (96%)
  local copies, waits for them, and re-layouts  0.66 us (3%)
    pallas_call x1, Pallas kernels, shards(): pl.pallas_call(functools.partial(kernel, n), out_shape=pltpu.VMEM((rows,...  23.3 us
    unnamed x1, local copies, waits for them, and re-layouts  0.66 us

profile of v2, /device:TPU:0, one launch (start us, length us, event | category | flops | bytes accessed | tf_op | source)
XLA Modules:
  0.0 24.0 jit_solution(13050474806456146662)
XLA Ops:
  0.0 23.3 %shard_map.64 = bf16[32,2048]{1,0:T(8,128)(2,1)S(1)} custom-call(bf16[32,2048]{1,0:T(8,128)(2,1)} %fk_ref.1, bf16[32,2048]{1,0:T(8,128)(2,1)} %sk_ref.1, bf16[32,2048]{1,0:T(8,128)(2,1)} %fv_ref.1, bf16[32,2048]{1,0:T(8,128)(2,1)} %sv_ref.1, bf16[32,2048]{1,0:T(8,128)(2,1)} %q_ref.1, s32[4]{0:T(128)} %sizes_hbm.1), custom_call_target="tpu_custom_call" | custom-call | tf_op jit(solution)/shard_map/pallas_call | solution.py:420
  23.3 0.7 %copy.8 = bf16[32,2048]{1,0:T(8,128)(2,1)} copy(bf16[32,2048]{1,0:T(8,128)(2,1)S(1)} %shard_map.64) | data formatting | bytes 262144

commit v3 on v2

--- a/solution.py
+++ b/solution.py
@@ -235,7 +235,7 @@
         to(peer, *kv_views(a, peer), kv_send.at[0], kv_recv.at[a]).start()
 
     def send_q(peer):
-        to(peer, *q_views(peer), q_send.at[0], q_recv.at[side]).start()
+        to(peer, *q_views(peer), q_send.at[0], q_recv.at[me // per]).start()
 
     def send_o(a, peer):
         to(peer, *o_views(a, peer), o_send.at[0], o_recv.at[0]).start()
@@ -277,21 +277,21 @@
             cores(t, (t >= 0) & (t < chips) & tied(t) & near(t), body)
 
     arrived(load_sem.at[0], stage)
+
     def met_q():
         send_q(buddy)
         met(send_q, True)
 
-    for a in range(held):
+    def met_kv(a):
         send_kv(a, buddy)
         met(functools.partial(send_kv, a), True)
-        if a == 0:
-            pl.when(side == 0)(met_q)
-    met(send_q, False)
 
     def first(target, cond):
         cores(target, cond & near(target), functools.partial(send_kv, 0))
         cores(target, cond & ((side == 0) | jnp.logical_not(near(target))), send_q)
 
+    met_kv(0)
+    pl.when(side == 0)(met_q)
     for e in range(1, chips):
         t = chip + e
         there = (t < chips) & jnp.logical_not(tied(t))
@@ -307,6 +307,9 @@
         if e == 2:
             t = chip + 1
             first(t, (t < chips) & tied(t))
+            met(send_q, False)
+            for a in range(1, held):
+                met_kv(a)
     for a in range(1, held):
         heard(functools.partial(send_kv, a))
 
@@ -332,14 +335,15 @@
         turned[a, :, 0:keys] = got_kv[a, 2].T
         turned[a, :, keys:2 * keys] = got_kv[a, 3].T
 
-    def attend(a, s):
-        token = s * keys + lax.broadcasted_iota(jnp.int32, (1, keys), 1)
-        limit = jnp.full((1, keys), 2 * keys, jnp.int32)
+    def attend(a, start, count):
+        at_q = slice(start, start + count)
+        token = start + lax.broadcasted_iota(jnp.int32, (1, count), 1)
+        limit = jnp.full((1, count), 2 * keys, jnp.int32)
         for e in reversed(ends):
             limit = jnp.where(token < e, e, limit)
-        fresh = lax.broadcasted_iota(jnp.int32, (keys, keys), 0) < limit - side * keys
+        fresh = lax.broadcasted_iota(jnp.int32, (keys, count), 0) < limit - side * keys
         both = got_kv[a, 0:2].reshape(2 * keys, hd)
-        qb = got_q[s * keys:(s + 1) * keys, a * hd:(a + 1) * hd]
+        qb = got_q[at_q, a * hd:(a + 1) * hd]
         x = lax.dot_general(both, qb, contract, preferred_element_type=jnp.float32)
         x = jnp.where(fresh, x[:keys], x[keys:])
         top = jnp.max(x, axis=0, keepdims=True)
@@ -349,41 +353,74 @@
         wf = jnp.where(fresh, w, zero).astype(jnp.bfloat16)
         ws = jnp.where(fresh, zero, w).astype(jnp.bfloat16)
         num = jnp.dot(turned[a], jnp.concatenate([wf, ws], axis=0), preferred_element_type=jnp.float32)
-        att[s * keys:(s + 1) * keys, a * hd:(a + 1) * hd] = (num * (1.0 / den)).T.astype(jnp.bfloat16)
+        att[at_q, a * hd:(a + 1) * hd] = (num * (1.0 / den)).T.astype(jnp.bfloat16)
         lse = top * scale + jnp.log2(den)
-        for b in range(keys // lanes):
-            lse_out[s * (keys // lanes) + b, a:a + 1, :] = lse[:, b * lanes:(b + 1) * lanes]
-
-    def give(s, body, own):
-        for j in range(s * half, (s + 1) * half):
-            pl.when(me != j)(functools.partial(body, j))
-        pl.when(side == s)(own)
-
-    def give_o(a, s):
-        give(s, functools.partial(send_o, a), lambda: keep(*o_views(a, me)))
-
-    def give_l(s):
-        give(s, send_l, lambda: keep(*l_views(me)))
-
-    def wait_q(s):
-        pl.when(side == s)(lambda: arrived(q_recv.at[s], got_q.at[0:(half - 1) * rows, :]))
-        pl.when(side != s)(lambda: arrived(q_recv.at[s], got_q.at[0:half * rows, :]))
-
-    for a in range(held):
+        for b in range(count // lanes):
+            lse_out[start // lanes + b, a:a + 1, :] = lse[:, b * lanes:(b + 1) * lanes]
+
+    def give(a, planes, last):
+        for p in planes:
+            for j in range(p * per, (p + 1) * per):
+                @pl.when(me != j)
+                def _(j=j):
+                    if last:
+                        send_l(j)
+                    send_o(a, j)
+
+    def own(a, last):
+        if last:
+            keep(*l_views(me))
+        keep(*o_views(a, me))
+
+    def work(a, planes, mine, last=False):
+        attend(a, planes[0] * lanes, len(planes) * lanes)
+        give(a, planes, last)
+        if mine:
+            own(a, last)
+
+    def wait_kv(a):
         arrived(kv_recv.at[a], got_kv.at[a, :, 0:(half - 1) * rows, :])
         turn(a)
-        if a == 0:
-            wait_q(0)
-        attend(a, 0)
-        if a == held - 1:
-            give_l(0)
-        give_o(a, 0)
-    wait_q(1)
-    for a in range(held):
-        attend(a, 1)
-        if a == held - 1:
-            give_l(1)
-        give_o(a, 1)
+
+    def wait_q(planes, mine):
+        for p in planes:
+            if mine:
+                pl.when(me // per == p)(lambda p=p: arrived(q_recv.at[p], got_q.at[0:(per - 1) * rows, :]))
+                pl.when(me // per != p)(lambda p=p: arrived(q_recv.at[p], got_q.at[0:per * rows, :]))
+            else:
+                arrived(q_recv.at[p], got_q.at[0:per * rows, :])
+
+    planes = n // per
+    low_planes, high_planes = range(planes // 2), range(planes // 2, planes)
+    end = held - 1
+
+    @pl.when(side == 0)
+    def _():
+        wait_kv(0)
+        wait_q(low_planes, True)
+        work(0, low_planes, True)
+        for p in high_planes[:-1]:
+            wait_q([p], False)
+            work(0, [p], False)
+        for a in range(1, held):
+            wait_kv(a)
+            work(a, low_planes, True, a == end)
+            for p in high_planes[:-1]:
+                work(a, [p], False, a == end)
+        wait_q(high_planes[-1:], False)
+        for a in range(held):
+            work(a, high_planes[-1:], False, a == end)
+
+    @pl.when(side == 1)
+    def _():
+        for a in range(held):
+            wait_kv(a)
+            if a == 0:
+                wait_q(low_planes, False)
+            work(a, low_planes, False, a == end)
+        wait_q(high_planes, True)
+        for a in range(held):
+            work(a, high_planes, True, a == end)
 
     most = (n - 1) * rows
     arrived(o_recv.at[0], att.at[0:most, :])
@@ -433,7 +470,7 @@
             pltpu.VMEM((n, held, lanes), jnp.float32),
             pltpu.VMEM((lanes, lanes), jnp.float32),
             pltpu.SMEM(patch_sizes.shape, patch_sizes.dtype),
-            dma((2,)), dma((held,)), dma((2,)), dma((1,)), dma((1,)),
+            dma((2,)), dma((held,)), dma((n * rows // lanes,)), dma((1,)), dma((1,)),
             dma((1,)), dma((1,)), dma((1,)), dma((1,)),
             pltpu.SemaphoreType.REGULAR((n // 2,)),
         ],

time: 24.2 us -> 23.2 us (0.959)
  the two profiles are of different devices: /device:TPU:0 before, /device:TPU:29 now
where the time goes in v3:
time: 23.2 us; the launch traced here: 23 us
  Pallas kernels  22.4 us (97%)
  local copies, waits for them, and re-layouts  0.66 us (3%)
    pallas_call x1, Pallas kernels, shards(): pl.pallas_call(functools.partial(kernel, n), out_shape=pltpu.VMEM((rows,...  22.4 us
    unnamed x1, local copies, waits for them, and re-layouts  0.66 us

profile of v3, /device:TPU:29, one launch (start us, length us, event | category | flops | bytes accessed | tf_op | source)
XLA Modules:
  0.0 23.0 jit_solution(5185029750967910922)
XLA Ops:
  0.0 22.4 %shard_map.64 = bf16[32,2048]{1,0:T(8,128)(2,1)S(1)} custom-call(bf16[32,2048]{1,0:T(8,128)(2,1)} %fk_ref.1, bf16[32,2048]{1,0:T(8,128)(2,1)} %sk_ref.1, bf16[32,2048]{1,0:T(8,128)(2,1)} %fv_ref.1, bf16[32,2048]{1,0:T(8,128)(2,1)} %sv_ref.1, bf16[32,2048]{1,0:T(8,128)(2,1)} %q_ref.1, s32[4]{0:T(128)} %sizes_hbm.1), custom_call_target="tpu_custom_call" | custom-call | tf_op jit(solution)/shard_map/pallas_call | solution.py:457
  22.4 0.7 %copy.8 = bf16[32,2048]{1,0:T(8,128)(2,1)} copy(bf16[32,2048]{1,0:T(8,128)(2,1)S(1)} %shard_map.64) | data formatting | bytes 262144

commit v4 on v3

--- a/solution.py
+++ b/solution.py
@@ -180,31 +180,39 @@
     lanes = lse_in.shape[2]
     per = lanes // rows
     chips = n // 2
-    side = me // half
 
     for i, ref in enumerate((fk_ref, sk_ref, fv_ref, sv_ref, q_ref)):
         pltpu.make_async_copy(ref, stage.at[i], load_sem.at[0]).start()
     load_sizes = pltpu.make_async_copy(sizes_hbm, sizes_ref, load_sem.at[1])
     load_sizes.start()
 
-    def wave(i):
-        return i // 4 + lax.rem(i // 2, 2)
-
     def signal(sem, peer):
         pl.semaphore_signal(sem, inc=1, device_id={"seq": peer}, device_id_type=MESH)
 
-    mine, chip = wave(me), me // 2
+    chip = lax.div(me, 2)
+    core = me - 2 * chip
+    side = lax.div(me, half)
+    place = chip - side * (chips // 2)
     upper = lax.rem(chip, 2) == 1
-    buddy = 2 * chip + 1 - lax.rem(me, 2)
+    buddy = 2 * chip + 1 - core
+
+    def wave(c):
+        return c // 2 + c % 2
+
+    mine = lax.div(chip + 1, 2)
     barrier = pltpu.get_barrier_semaphore()
     signal(barrier, buddy)
-    for d in range(1, n):
-        peer = me + d
-        pl.when((peer < n) & (wave(peer) > mine))(functools.partial(signal, barrier, jnp.where(peer < n, peer, me)))
+    for t in range(1, chips):
+        @pl.when(mine < wave(t))
+        def _():
+            signal(barrier, 2 * t)
+            signal(barrier, 2 * t + 1)
     pl.semaphore_wait(barrier, jnp.maximum(4 * mine - 2, 0) + 1)
-    for d in range(1, n):
-        peer = me - d
-        pl.when((peer >= 0) & (wave(peer) < mine))(functools.partial(signal, ready.at[chip], jnp.maximum(peer, 0)))
+    for t in range(chips - 2, -1, -1):
+        @pl.when(mine > wave(t))
+        def _():
+            signal(ready.at[chip], 2 * t)
+            signal(ready.at[chip], 2 * t + 1)
 
     def cols(h, count=1):
         return pl.ds(pl.multiple_of(h * hd, hd), count * hd)
@@ -217,25 +225,25 @@
             src_ref=src, dst_ref=dst, send_sem=send, recv_sem=recv,
             device_id={"seq": peer}, device_id_type=MESH)
 
+    local = me - side * half
+
     def kv_views(a, peer):
-        return (stage.at[0:4, :, cols(lax.rem(peer, half) * held + a)],
-                got_kv.at[a, :, at(lax.rem(me, half)), :])
-
-    def q_views(peer):
-        return stage.at[4, :, cols(lax.rem(peer, half) * held, held)], got_q.at[at(me), :]
+        return (stage.at[0:4, :, cols((peer - side * half) * held + a)], got_kv.at[a, :, at(local), :])
+
+    def q_views(peer, base):
+        return stage.at[4, :, cols((peer - base) * held, held)], got_q.at[at(me), :]
 
     def o_views(a, peer):
-        return (att.at[at(peer), a * hd:(a + 1) * hd],
-                part.at[side, :, cols(lax.rem(me, half) * held + a)])
+        return att.at[at(peer), a * hd:(a + 1) * hd], part.at[side, :, cols(local * held + a)]
 
     def l_views(peer):
-        return lse_out.at[peer // per], lse_in.at[me]
+        return lse_out.at[peer // per if isinstance(peer, int) else lax.div(peer, per)], lse_in.at[me]
 
     def send_kv(a, peer):
         to(peer, *kv_views(a, peer), kv_send.at[0], kv_recv.at[a]).start()
 
-    def send_q(peer):
-        to(peer, *q_views(peer), q_send.at[0], q_recv.at[me // per]).start()
+    def send_q(base, peer):
+        to(peer, *q_views(peer, base), q_send.at[0], q_recv.at[lax.div(me, per)]).start()
 
     def send_o(a, peer):
         to(peer, *o_views(a, peer), o_send.at[0], o_recv.at[0]).start()
@@ -252,75 +260,70 @@
     def keep(src, dst):
         dst[...] = src[...]
 
-    def cores(target, cond, body):
-        @pl.when(cond)
+    def cores(target, body):
+        body(2 * target)
+        body(2 * target + 1)
+
+    def hear(target):
+        pl.semaphore_wait(ready.at[target], 2)
+
+    quad = chips // 2
+
+    def nears(body):
+        for e in range(quad - 1, 0, -1):
+            pl.when(place >= e)(lambda: cores(chip - e, body))
+            pl.when(place + e < quad)(lambda: cores(chip + e, body))
+
+    arrived(load_sem.at[0], stage)
+    head_a = functools.partial(send_kv, 0)
+    head_a(buddy)
+    for e in range(1, quad):
+        there = place >= e
+        pl.when(there & upper if e == 1 else there)(lambda: cores(chip - e, head_a))
+    for e in range(1, quad):
+        there = place + e < quad
+
+        @pl.when(there & jnp.logical_not(upper) if e == 1 else there)
         def _():
-            for core in range(2):
-                body(2 * jnp.clip(target, 0, chips - 1) + core)
-
-    def near(target):
-        return target // (chips // 2) == side
-
-    def tied(target):
-        return (upper & (target == chip + 1)) | (jnp.logical_not(upper) & (target == chip - 1))
-
-    def met(body, same):
-        for e in range(1, chips):
-            t = chip - e
-            cores(t, (t >= 0) & jnp.logical_not(tied(t)) & (near(t) == same), body)
-
-    def heard(body):
-        for e in range(1, chips):
-            t = chip + e
-            cores(t, (t < chips) & jnp.logical_not(tied(t)) & near(t), body)
-        for t in (chip - 1, chip + 1):
-            cores(t, (t >= 0) & (t < chips) & tied(t) & near(t), body)
-
-    arrived(load_sem.at[0], stage)
-
-    def met_q():
-        send_q(buddy)
-        met(send_q, True)
-
-    def met_kv(a):
+            hear(chip + e)
+            cores(chip + e, head_a)
+
+        if e == 1:
+            pl.when((place >= 1) & jnp.logical_not(upper))(lambda: cores(chip - 1, head_a))
+        if e == 2:
+            pl.when((place + 1 < quad) & upper)(lambda: cores(chip + 1, head_a))
+
+    @pl.when(side == 1)
+    def _():
+        for t in range(quad):
+            cores(t, functools.partial(send_q, 0))
+
+    @pl.when(side == 0)
+    def _():
+        edge = chip == quad - 1
+        far = functools.partial(send_q, half)
+        for t in range(quad, chips):
+            @pl.when(jnp.logical_not(edge) if t == quad else side == 0)
+            def _():
+                hear(t)
+                cores(t, far)
+
+            if t == quad + 1:
+                pl.when(edge)(lambda: cores(quad, far))
+
+    def send_near_q():
+        near_q = functools.partial(send_q, side * half)
+        near_q(buddy)
+        nears(near_q)
+
+    pl.when(side == 0)(send_near_q)
+    for a in range(1, held):
         send_kv(a, buddy)
-        met(functools.partial(send_kv, a), True)
-
-    def first(target, cond):
-        cores(target, cond & near(target), functools.partial(send_kv, 0))
-        cores(target, cond & ((side == 0) | jnp.logical_not(near(target))), send_q)
-
-    met_kv(0)
-    pl.when(side == 0)(met_q)
-    for e in range(1, chips):
-        t = chip + e
-        there = (t < chips) & jnp.logical_not(tied(t))
-
-        @pl.when(there)
-        def _():
-            pl.semaphore_wait(ready.at[t], 2)
-
-        first(t, there)
-        if e == 1:
-            t = chip - 1
-            first(t, (t >= 0) & tied(t))
-        if e == 2:
-            t = chip + 1
-            first(t, (t < chips) & tied(t))
-            met(send_q, False)
-            for a in range(1, held):
-                met_kv(a)
-    for a in range(1, held):
-        heard(functools.partial(send_kv, a))
-
-    def late_q():
-        met_q()
-        heard(send_q)
-
-    pl.when(side == 1)(late_q)
+        nears(functools.partial(send_kv, a))
+    pl.when(side == 1)(send_near_q)
     for a in range(held):
         keep(*kv_views(a, me))
-    keep(*q_views(me))
+    keep(*q_views(me, side * half))
     load_sizes.wait()
 
     ends, total = [], 0
@@ -385,8 +388,8 @@
     def wait_q(planes, mine):
         for p in planes:
             if mine:
-                pl.when(me // per == p)(lambda p=p: arrived(q_recv.at[p], got_q.at[0:(per - 1) * rows, :]))
-                pl.when(me // per != p)(lambda p=p: arrived(q_recv.at[p], got_q.at[0:per * rows, :]))
+                pl.when(lax.div(me, per) == p)(lambda p=p: arrived(q_recv.at[p], got_q.at[0:(per - 1) * rows, :]))
+                pl.when(lax.div(me, per) != p)(lambda p=p: arrived(q_recv.at[p], got_q.at[0:per * rows, :]))
             else:
                 arrived(q_recv.at[p], got_q.at[0:per * rows, :])
 
@@ -397,19 +400,15 @@
     @pl.when(side == 0)
     def _():
         wait_kv(0)
+        for p in high_planes:
+            wait_q([p], False)
+            work(0, [p], False)
         wait_q(low_planes, True)
         work(0, low_planes, True)
-        for p in high_planes[:-1]:
-            wait_q([p], False)
-            work(0, [p], False)
         for a in range(1, held):
             wait_kv(a)
             work(a, low_planes, True, a == end)
-            for p in high_planes[:-1]:
-                work(a, [p], False, a == end)
-        wait_q(high_planes[-1:], False)
-        for a in range(held):
-            work(a, high_planes[-1:], False, a == end)
+            work(a, high_planes, False, a == end)
 
     @pl.when(side == 1)
     def _():

time: 23.2 us -> 22.4 us (0.966)
  the two profiles are of different devices: /device:TPU:29 before, /device:TPU:0 now
where the time goes in v4:
time: 22.4 us; the launch traced here: 22.2 us
  Pallas kernels  21.6 us (96%)
  local copies, waits for them, and re-layouts  0.66 us (3%)
    pallas_call x1, Pallas kernels, shards(): pl.pallas_call(functools.partial(kernel, n), out_shape=pltpu.VMEM((rows,...  21.6 us
    unnamed x1, local copies, waits for them, and re-layouts  0.66 us

profile of v4, /device:TPU:0, one launch (start us, length us, event | category | flops | bytes accessed | tf_op | source)
XLA Modules:
  0.0 22.2 jit_solution(12178107252549949314)
XLA Ops:
  0.0 21.6 %shard_map.64 = bf16[32,2048]{1,0:T(8,128)(2,1)S(1)} custom-call(bf16[32,2048]{1,0:T(8,128)(2,1)} %fk_ref.1, bf16[32,2048]{1,0:T(8,128)(2,1)} %sk_ref.1, bf16[32,2048]{1,0:T(8,128)(2,1)} %fv_ref.1, bf16[32,2048]{1,0:T(8,128)(2,1)} %sv_ref.1, bf16[32,2048]{1,0:T(8,128)(2,1)} %q_ref.1, s32[4]{0:T(128)} %sizes_hbm.1), custom_call_target="tpu_custom_call" | custom-call | tf_op jit(solution)/shard_map/pallas_call | solution.py:456
  21.6 0.7 %copy.8 = bf16[32,2048]{1,0:T(8,128)(2,1)} copy(bf16[32,2048]{1,0:T(8,128)(2,1)S(1)} %shard_map.64) | data formatting | bytes 262144

commit v5 on v4

--- a/solution.py
+++ b/solution.py
@@ -182,8 +182,10 @@
     chips = n // 2
 
     for i, ref in enumerate((fk_ref, sk_ref, fv_ref, sv_ref, q_ref)):
-        pltpu.make_async_copy(ref, stage.at[i], load_sem.at[0]).start()
-    load_sizes = pltpu.make_async_copy(sizes_hbm, sizes_ref, load_sem.at[1])
+        for r in range(0, rows, 16):
+            piece = pl.ds(r, min(16, rows))
+            pltpu.make_async_copy(ref.at[piece, :], stage.at[i, piece, :], load_sem.at[i // 4]).start()
+    load_sizes = pltpu.make_async_copy(sizes_hbm, sizes_ref, load_sem.at[2])
     load_sizes.start()
 
     def signal(sem, peer):
@@ -196,23 +198,26 @@
     upper = lax.rem(chip, 2) == 1
     buddy = 2 * chip + 1 - core
 
-    def wave(c):
-        return c // 2 + c % 2
-
-    mine = lax.div(chip + 1, 2)
+    floor = lax.div(chip, 2)
     barrier = pltpu.get_barrier_semaphore()
     signal(barrier, buddy)
+
+    def tell(sem, target):
+        signal(sem, 2 * target)
+        signal(sem, 2 * target + 1)
+
     for t in range(1, chips):
-        @pl.when(mine < wave(t))
-        def _():
-            signal(barrier, 2 * t)
-            signal(barrier, 2 * t + 1)
-    pl.semaphore_wait(barrier, jnp.maximum(4 * mine - 2, 0) + 1)
+        later = floor < t // 2
+        if t % 2:
+            pl.when(later | ((chip < t) & jnp.logical_not(upper)))(functools.partial(tell, barrier, t))
+        else:
+            pl.when(later & jnp.logical_not(upper))(functools.partial(tell, barrier, t))
+    pl.semaphore_wait(barrier, jnp.where(upper, 4 * floor + 3, 2 * floor + 1))
     for t in range(chips - 2, -1, -1):
-        @pl.when(mine > wave(t))
-        def _():
-            signal(ready.at[chip], 2 * t)
-            signal(ready.at[chip], 2 * t + 1)
+        if t % 2:
+            pl.when((chip > t) & upper)(functools.partial(tell, ready.at[chip], t))
+        else:
+            pl.when((floor > t // 2) | ((chip > t) & upper))(functools.partial(tell, ready.at[chip], t))
 
     def cols(h, count=1):
         return pl.ds(pl.multiple_of(h * hd, hd), count * hd)
@@ -246,7 +251,7 @@
         to(peer, *q_views(peer, base), q_send.at[0], q_recv.at[lax.div(me, per)]).start()
 
     def send_o(a, peer):
-        to(peer, *o_views(a, peer), o_send.at[0], o_recv.at[0]).start()
+        to(peer, *o_views(a, peer), o_send.at[0], o_recv.at[a]).start()
 
     def send_l(peer):
         to(peer, *l_views(peer), l_send.at[0], l_recv.at[0]).start()
@@ -269,29 +274,44 @@
 
     quad = chips // 2
 
+    first = side * quad
+    across = 2 * first + quad - 1 - chip
+    along = first + lax.rem(place + 2, quad)
+    beside = chip + 1 - 2 * lax.rem(chip, 2)
+
     def nears(body):
-        for e in range(quad - 1, 0, -1):
-            pl.when(place >= e)(lambda: cores(chip - e, body))
-            pl.when(place + e < quad)(lambda: cores(chip + e, body))
-
-    arrived(load_sem.at[0], stage)
+        for target in (across, along, beside):
+            cores(target, body)
+
+    arrived(load_sem.at[0], stage.at[0:4])
     head_a = functools.partial(send_kv, 0)
     head_a(buddy)
-    for e in range(1, quad):
-        there = place >= e
-        pl.when(there & upper if e == 1 else there)(lambda: cores(chip - e, head_a))
-    for e in range(1, quad):
-        there = place + e < quad
-
-        @pl.when(there & jnp.logical_not(upper) if e == 1 else there)
-        def _():
-            hear(chip + e)
-            cores(chip + e, head_a)
-
-        if e == 1:
-            pl.when((place >= 1) & jnp.logical_not(upper))(lambda: cores(chip - 1, head_a))
-        if e == 2:
-            pl.when((place + 1 < quad) & upper)(lambda: cores(chip + 1, head_a))
+
+    @pl.when(place == 0)
+    def _():
+        for target in (beside, along, across):
+            hear(target)
+            cores(target, head_a)
+
+    @pl.when(place == 1)
+    def _():
+        cores(beside, head_a)
+        hear(along)
+        cores(across, head_a)
+        cores(along, head_a)
+
+    @pl.when(place == 2)
+    def _():
+        cores(along, head_a)
+        hear(beside)
+        cores(across, head_a)
+        cores(beside, head_a)
+
+    @pl.when(place == 3)
+    def _():
+        nears(head_a)
+
+    arrived(load_sem.at[1], stage.at[4])
 
     @pl.when(side == 1)
     def _():
@@ -300,16 +320,20 @@
 
     @pl.when(side == 0)
     def _():
-        edge = chip == quad - 1
         far = functools.partial(send_q, half)
-        for t in range(quad, chips):
-            @pl.when(jnp.logical_not(edge) if t == quad else side == 0)
+        for t in range(quad, chips, 2):
+            @pl.when(jnp.logical_not(upper))
             def _():
                 hear(t)
                 cores(t, far)
-
-            if t == quad + 1:
-                pl.when(edge)(lambda: cores(quad, far))
+                hear(t + 1)
+                cores(t + 1, far)
+
+            @pl.when(upper)
+            def _():
+                hear(t + 1)
+                cores(t + 1, far)
+                cores(t, far)
 
     def send_near_q():
         near_q = functools.partial(send_q, side * half)
@@ -362,7 +386,7 @@
             lse_out[start // lanes + b, a:a + 1, :] = lse[:, b * lanes:(b + 1) * lanes]
 
     def give(a, planes, last):
-        for p in planes:
+        for p in planes if planes[0] < n // per // 2 else reversed(planes):
             for j in range(p * per, (p + 1) * per):
                 @pl.when(me != j)
                 def _(j=j):
@@ -422,7 +446,6 @@
             work(a, high_planes, True, a == end)
 
     most = (n - 1) * rows
-    arrived(o_recv.at[0], att.at[0:most, :])
     arrived(l_recv.at[0], lse_in.at[0:n - 1])
     low = lse_in[0:half].reshape(H, lanes)
     high = lse_in[half:n].reshape(H, lanes)
@@ -432,11 +455,13 @@
     fill = jnp.zeros((lanes - 2 * H, lanes), jnp.float32)
     mix[...] = jnp.concatenate([low / total, high / total, fill], axis=0).T
     share = mix[at(lax.rem(me, per)), :]
-    for h in range(H):
-        c = slice(h * hd, (h + 1) * hd)
-        out = share[:, h:h + 1] * part[0, :, c].astype(jnp.float32)
-        out = out + share[:, H + h:H + h + 1] * part[1, :, c].astype(jnp.float32)
-        out_ref[:, c] = out.astype(out_ref.dtype)
+    for a in range(held):
+        arrived(o_recv.at[a], att.at[0:most, 0:hd])
+        for h in range(a, H, held):
+            c = slice(h * hd, (h + 1) * hd)
+            out = share[:, h:h + 1] * part[0, :, c].astype(jnp.float32)
+            out = out + share[:, H + h:H + h + 1] * part[1, :, c].astype(jnp.float32)
+            out_ref[:, c] = out.astype(out_ref.dtype)
 
     left(kv_send.at[0], got_kv.at[:, :, 0:(half - 1) * rows, :])
     left(q_send.at[0], got_q.at[0:most, :])
@@ -469,7 +494,7 @@
             pltpu.VMEM((n, held, lanes), jnp.float32),
             pltpu.VMEM((lanes, lanes), jnp.float32),
             pltpu.SMEM(patch_sizes.shape, patch_sizes.dtype),
-            dma((2,)), dma((held,)), dma((n * rows // lanes,)), dma((1,)), dma((1,)),
+            dma((3,)), dma((held,)), dma((n * rows // lanes,)), dma((held,)), dma((1,)),
             dma((1,)), dma((1,)), dma((1,)), dma((1,)),
             pltpu.SemaphoreType.REGULAR((n // 2,)),
         ],

time: 22.4 us -> 21.9 us (0.978)
  Pallas kernels: 21.6 us -> 21 us
    pallas_call x1, Pallas kernels: 21.6 us -> 21 us  [shards(): pl.pallas_call(functools.partial(kernel, n), out_shape=pltpu.VMEM((rows,...]
where the time goes in v5:
time: 21.9 us; the launch traced here: 21.6 us
  Pallas kernels  21 us (96%)
  local copies, waits for them, and re-layouts  0.66 us (3%)
    pallas_call x1, Pallas kernels, shards(): pl.pallas_call(functools.partial(kernel, n), out_shape=pltpu.VMEM((rows,...  21 us
    unnamed x1, local copies, waits for them, and re-layouts  0.66 us

profile of v5, /device:TPU:0, one launch (start us, length us, event | category | flops | bytes accessed | tf_op | source)
XLA Modules:
  0.0 21.6 jit_solution(1009591656886619325)
XLA Ops:
  0.0 21.0 %shard_map.64 = bf16[32,2048]{1,0:T(8,128)(2,1)S(1)} custom-call(bf16[32,2048]{1,0:T(8,128)(2,1)} %fk_ref.1, bf16[32,2048]{1,0:T(8,128)(2,1)} %sk_ref.1, bf16[32,2048]{1,0:T(8,128)(2,1)} %fv_ref.1, bf16[32,2048]{1,0:T(8,128)(2,1)} %sv_ref.1, bf16[32,2048]{1,0:T(8,128)(2,1)} %q_ref.1, s32[4]{0:T(128)} %sizes_hbm.1), custom_call_target="tpu_custom_call" | custom-call | tf_op jit(solution)/shard_map/pallas_call | solution.py:481
  21.0 0.7 %copy.8 = bf16[32,2048]{1,0:T(8,128)(2,1)} copy(bf16[32,2048]{1,0:T(8,128)(2,1)S(1)} %shard_map.64) | data formatting | bytes 262144

commit v6 on v5

--- a/solution.py
+++ b/solution.py
@@ -215,9 +215,9 @@
     pl.semaphore_wait(barrier, jnp.where(upper, 4 * floor + 3, 2 * floor + 1))
     for t in range(chips - 2, -1, -1):
         if t % 2:
-            pl.when((chip > t) & upper)(functools.partial(tell, ready.at[chip], t))
+            pl.when((core == 1) & (chip > t) & upper)(functools.partial(tell, ready.at[chip], t))
         else:
-            pl.when((floor > t // 2) | ((chip > t) & upper))(functools.partial(tell, ready.at[chip], t))
+            pl.when((core == 1) & ((floor > t // 2) | ((chip > t) & upper)))(functools.partial(tell, ready.at[chip], t))
 
     def cols(h, count=1):
         return pl.ds(pl.multiple_of(h * hd, hd), count * hd)
@@ -270,7 +270,7 @@
         body(2 * target + 1)
 
     def hear(target):
-        pl.semaphore_wait(ready.at[target], 2)
+        pl.semaphore_wait(ready.at[target], 1)
 
     quad = chips // 2
 
@@ -280,7 +280,8 @@
     beside = chip + 1 - 2 * lax.rem(chip, 2)
 
     def nears(body):
-        for target in (across, along, beside):
+        swap = place == 1
+        for target in (jnp.where(swap, along, across), jnp.where(swap, across, along), beside):
             cores(target, body)
 
     arrived(load_sem.at[0], stage.at[0:4])
@@ -313,10 +314,23 @@
 
     arrived(load_sem.at[1], stage.at[4])
 
-    @pl.when(side == 1)
+    last_plane = n // per - 1
+
+    def send_one(a, peer):
+        src = stage.at[4, :, cols(peer * held + a)]
+        dst = got_q.at[at(me), a * hd:(a + 1) * hd]
+        to(peer, src, dst, q_send.at[0], q_recv.at[last_plane + a]).start()
+
+    @pl.when((side == 1) & (place < 2))
     def _():
         for t in range(quad):
             cores(t, functools.partial(send_q, 0))
+
+    def send_low(a):
+        for t in range(quad):
+            cores(t, functools.partial(send_one, a))
+
+    pl.when((side == 1) & (place >= 2))(functools.partial(send_low, 0))
 
     @pl.when(side == 0)
     def _():
@@ -344,6 +358,8 @@
     for a in range(1, held):
         send_kv(a, buddy)
         nears(functools.partial(send_kv, a))
+    for a in range(1, held):
+        pl.when((side == 1) & (place >= 2))(functools.partial(send_low, a))
     pl.when(side == 1)(send_near_q)
     for a in range(held):
         keep(*kv_views(a, me))
@@ -417,6 +433,9 @@
             else:
                 arrived(q_recv.at[p], got_q.at[0:per * rows, :])
 
+    def wait_one(a):
+        arrived(q_recv.at[last_plane + a], got_q.at[0:per * rows, 0:hd])
+
     planes = n // per
     low_planes, high_planes = range(planes // 2), range(planes // 2, planes)
     end = held - 1
@@ -424,14 +443,17 @@
     @pl.when(side == 0)
     def _():
         wait_kv(0)
-        for p in high_planes:
-            wait_q([p], False)
-            work(0, [p], False)
+        wait_q(high_planes[:1], False)
+        work(0, high_planes[:1], False)
         wait_q(low_planes, True)
         work(0, low_planes, True)
+        last = high_planes[-1:]
+        wait_one(0)
+        work(0, last, False)
         for a in range(1, held):
             wait_kv(a)
             work(a, low_planes, True, a == end)
+            wait_one(a)
             work(a, high_planes, False, a == end)
 
     @pl.when(side == 1)
@@ -494,7 +516,7 @@
             pltpu.VMEM((n, held, lanes), jnp.float32),
             pltpu.VMEM((lanes, lanes), jnp.float32),
             pltpu.SMEM(patch_sizes.shape, patch_sizes.dtype),
-            dma((3,)), dma((held,)), dma((n * rows // lanes,)), dma((held,)), dma((1,)),
+            dma((3,)), dma((held,)), dma((n * rows // lanes + held - 1,)), dma((held,)), dma((1,)),
             dma((1,)), dma((1,)), dma((1,)), dma((1,)),
             pltpu.SemaphoreType.REGULAR((n // 2,)),
         ],

time: 21.9 us -> 21.9 us (level)
  no operation moved by 1% of the time
where the time goes in v6:
time: 21.9 us; the launch traced here: 21.7 us
  Pallas kernels  21 us (96%)
  local copies, waits for them, and re-layouts  0.66 us (3%)
    pallas_call x1, Pallas kernels, shards(): pl.pallas_call(functools.partial(kernel, n), out_shape=pltpu.VMEM((rows,...  21 us
    unnamed x1, local copies, waits for them, and re-layouts  0.66 us

profile of v6, /device:TPU:0, one launch (start us, length us, event | category | flops | bytes accessed | tf_op | source)
XLA Modules:
  0.0 21.7 jit_solution(6913016378768216799)
XLA Ops:
  0.0 21.0 %shard_map.64 = bf16[32,2048]{1,0:T(8,128)(2,1)S(1)} custom-call(bf16[32,2048]{1,0:T(8,128)(2,1)} %fk_ref.1, bf16[32,2048]{1,0:T(8,128)(2,1)} %sk_ref.1, bf16[32,2048]{1,0:T(8,128)(2,1)} %fv_ref.1, bf16[32,2048]{1,0:T(8,128)(2,1)} %sv_ref.1, bf16[32,2048]{1,0:T(8,128)(2,1)} %q_ref.1, s32[4]{0:T(128)} %sizes_hbm.1), custom_call_target="tpu_custom_call" | custom-call | tf_op jit(solution)/shard_map/pallas_call | solution.py:503
  21.1 0.7 %copy.8 = bf16[32,2048]{1,0:T(8,128)(2,1)} copy(bf16[32,2048]{1,0:T(8,128)(2,1)S(1)} %shard_map.64) | data formatting | bytes 262144

commit v7 on v6

--- a/solution.py
+++ b/solution.py
@@ -336,18 +336,27 @@
     def _():
         far = functools.partial(send_q, half)
         for t in range(quad, chips, 2):
+            now = place < (2 if t + 2 == chips else quad)
+
             @pl.when(jnp.logical_not(upper))
             def _():
                 hear(t)
-                cores(t, far)
+                pl.when(now)(lambda: cores(t, far))
                 hear(t + 1)
-                cores(t + 1, far)
+                pl.when(now)(lambda: cores(t + 1, far))
 
             @pl.when(upper)
             def _():
                 hear(t + 1)
-                cores(t + 1, far)
-                cores(t, far)
+
+                @pl.when(now)
+                def _():
+                    cores(t + 1, far)
+                    cores(t, far)
+
+    def send_top_q():
+        for t in (chips - 2, chips - 1):
+            cores(t, functools.partial(send_q, half))
 
     def send_near_q():
         near_q = functools.partial(send_q, side * half)
@@ -443,6 +452,7 @@
     @pl.when(side == 0)
     def _():
         wait_kv(0)
+        pl.when(place >= 2)(send_top_q)
         wait_q(high_planes[:1], False)
         work(0, high_planes[:1], False)
         wait_q(low_planes, True)
@@ -458,11 +468,13 @@
 
     @pl.when(side == 1)
     def _():
-        for a in range(held):
-            wait_kv(a)
-            if a == 0:
-                wait_q(low_planes, False)
-            work(a, low_planes, False, a == end)
+        for p in low_planes:
+            for a in range(held):
+                if p == 0:
+                    wait_kv(a)
+                if a == 0:
+                    wait_q([p], False)
+                work(a, [p], False, a == end)
         wait_q(high_planes, True)
         for a in range(held):
             work(a, high_planes, True, a == end)

time: 21.9 us -> 21.5 us (0.982)
  Pallas kernels: 21 us -> 20.5 us
    pallas_call x1, Pallas kernels: 21 us -> 20.5 us  [shards(): pl.pallas_call(functools.partial(kernel, n), out_shape=pltpu.VMEM((rows,...]
where the time goes in v7:
time: 21.5 us; the launch traced here: 21.2 us
  Pallas kernels  20.5 us (95%)
  local copies, waits for them, and re-layouts  0.66 us (3%)
    pallas_call x1, Pallas kernels, shards(): pl.pallas_call(functools.partial(kernel, n), out_shape=pltpu.VMEM((rows,...  20.5 us
    unnamed x1, local copies, waits for them, and re-layouts  0.66 us

profile of v7, /device:TPU:0, one launch (start us, length us, event | category | flops | bytes accessed | tf_op | source)
XLA Modules:
  0.0 21.2 jit_solution(14575615798674103227)
XLA Ops:
  0.0 20.5 %shard_map.64 = bf16[32,2048]{1,0:T(8,128)(2,1)S(1)} custom-call(bf16[32,2048]{1,0:T(8,128)(2,1)} %fk_ref.1, bf16[32,2048]{1,0:T(8,128)(2,1)} %sk_ref.1, bf16[32,2048]{1,0:T(8,128)(2,1)} %fv_ref.1, bf16[32,2048]{1,0:T(8,128)(2,1)} %sv_ref.1, bf16[32,2048]{1,0:T(8,128)(2,1)} %q_ref.1, s32[4]{0:T(128)} %sizes_hbm.1), custom_call_target="tpu_custom_call" | custom-call | tf_op jit(solution)/shard_map/pallas_call | solution.py:515
  20.5 0.7 %copy.8 = bf16[32,2048]{1,0:T(8,128)(2,1)} copy(bf16[32,2048]{1,0:T(8,128)(2,1)S(1)} %shard_map.64) | data formatting | bytes 262144

commit v8 on v7

--- a/solution.py
+++ b/solution.py
@@ -468,13 +468,24 @@
 
     @pl.when(side == 1)
     def _():
-        for p in low_planes:
+        @pl.when(place < 2)
+        def _():
             for a in range(held):
-                if p == 0:
-                    wait_kv(a)
+                wait_kv(a)
                 if a == 0:
-                    wait_q([p], False)
-                work(a, [p], False, a == end)
+                    wait_q(low_planes, False)
+                work(a, low_planes, False, a == end)
+
+        @pl.when(place >= 2)
+        def _():
+            for p in low_planes:
+                for a in range(held):
+                    if p == 0:
+                        wait_kv(a)
+                    if a == 0:
+                        wait_q([p], False)
+                    work(a, [p], False, a == end)
+
         wait_q(high_planes, True)
         for a in range(held):
             work(a, high_planes, True, a == end)

time: 21.5 us -> 21.5 us (level)
  no operation moved by 1% of the time
where the time goes in v8:
time: 21.5 us; the launch traced here: 21.2 us
  Pallas kernels  20.5 us (95%)
  local copies, waits for them, and re-layouts  0.66 us (3%)
    pallas_call x1, Pallas kernels, shards(): pl.pallas_call(functools.partial(kernel, n), out_shape=pltpu.VMEM((rows,...  20.5 us
    unnamed x1, local copies, waits for them, and re-layouts  0.66 us

profile of v8, /device:TPU:0, one launch (start us, length us, event | category | flops | bytes accessed | tf_op | source)
XLA Modules:
  0.0 21.2 jit_solution(15101646169495751859)
XLA Ops:
  0.0 20.5 %shard_map.64 = bf16[32,2048]{1,0:T(8,128)(2,1)S(1)} custom-call(bf16[32,2048]{1,0:T(8,128)(2,1)} %fk_ref.1, bf16[32,2048]{1,0:T(8,128)(2,1)} %sk_ref.1, bf16[32,2048]{1,0:T(8,128)(2,1)} %fv_ref.1, bf16[32,2048]{1,0:T(8,128)(2,1)} %sv_ref.1, bf16[32,2048]{1,0:T(8,128)(2,1)} %q_ref.1, s32[4]{0:T(128)} %sizes_hbm.1), custom_call_target="tpu_custom_call" | custom-call | tf_op jit(solution)/shard_map/pallas_call | solution.py:526
  20.5 0.7 %copy.8 = bf16[32,2048]{1,0:T(8,128)(2,1)} copy(bf16[32,2048]{1,0:T(8,128)(2,1)S(1)} %shard_map.64) | data formatting | bytes 262144

commit v9 on v8

--- a/solution.py
+++ b/solution.py
@@ -410,8 +410,8 @@
         for b in range(count // lanes):
             lse_out[start // lanes + b, a:a + 1, :] = lse[:, b * lanes:(b + 1) * lanes]
 
-    def give(a, planes, last):
-        for p in planes if planes[0] < n // per // 2 else reversed(planes):
+    def give(a, planes, last, turned_round):
+        for p in reversed(planes) if turned_round else planes:
             for j in range(p * per, (p + 1) * per):
                 @pl.when(me != j)
                 def _(j=j):
@@ -426,7 +426,7 @@
 
     def work(a, planes, mine, last=False):
         attend(a, planes[0] * lanes, len(planes) * lanes)
-        give(a, planes, last)
+        give(a, planes, last, not mine and planes[0] > 0)
         if mine:
             own(a, last)
 

time: 21.5 us -> 21.5 us (level)
  no operation moved by 1% of the time
where the time goes in v9:
time: 21.5 us; the launch traced here: 21.2 us
  Pallas kernels  20.5 us (95%)
  local copies, waits for them, and re-layouts  0.66 us (3%)
    pallas_call x1, Pallas kernels, shards(): pl.pallas_call(functools.partial(kernel, n), out_shape=pltpu.VMEM((rows,...  20.5 us
    unnamed x1, local copies, waits for them, and re-layouts  0.66 us

profile of v9, /device:TPU:0, one launch (start us, length us, event | category | flops | bytes accessed | tf_op | source)
XLA Modules:
  0.0 21.2 jit_solution(3826938910821167302)
XLA Ops:
  0.0 20.5 %shard_map.64 = bf16[32,2048]{1,0:T(8,128)(2,1)S(1)} custom-call(bf16[32,2048]{1,0:T(8,128)(2,1)} %fk_ref.1, bf16[32,2048]{1,0:T(8,128)(2,1)} %sk_ref.1, bf16[32,2048]{1,0:T(8,128)(2,1)} %fv_ref.1, bf16[32,2048]{1,0:T(8,128)(2,1)} %sv_ref.1, bf16[32,2048]{1,0:T(8,128)(2,1)} %q_ref.1, s32[4]{0:T(128)} %sizes_hbm.1), custom_call_target="tpu_custom_call" | custom-call | tf_op jit(solution)/shard_map/pallas_call | solution.py:526
  20.5 0.7 %copy.8 = bf16[32,2048]{1,0:T(8,128)(2,1)} copy(bf16[32,2048]{1,0:T(8,128)(2,1)S(1)} %shard_map.64) | data formatting | bytes 262144
